TPU v7x, 32 devices: a whole 2x2x4 slice. The times are simulated.
32 devices in a mesh: groups: 2 (over y), expert: 4 (over x, core), etp: 4 (over z).
Axes of the slice: x: 2, y: 2, z: 4, core: 2. Of those that a mesh axis runs over, the one named last changes fastest.
Arguments:
- tokens: bfloat16 [1024, 4096], P(('groups', 'expert'), 'etp'), parts along dimension 0, may hold values from -6 to 6
- route_ids: int32 [1024, 2], P(('groups', 'expert')), parts along dimension 0, may hold values from 0 to 3, all different within a row; in each aligned block of 128 rows (0 to 127, 128 to 255, ...) at most 96 rows name the same one
- gate_weights: float32 [1024, 2], P(('groups', 'expert')), parts along dimension 0, may hold values from 0.2 to 1
- w_gate: bfloat16 [4, 4096, 14336], P('expert', None, 'etp'), may hold values from -0.09375 to 0.09375
- w_up: bfloat16 [4, 4096, 14336], P('expert', None, 'etp'), may hold values from -0.09375 to 0.09375
- w_down: bfloat16 [4, 14336, 4096], P('expert', 'etp'), may hold values from -0.0625 to 0.0625
Outputs:
- mixed: bfloat16 [1024, 4096], P(('groups', 'expert'), 'etp'), parts along dimension 0
There are 2 independent parts, one for each index of `groups`. A program takes and returns all parts, laid end to end along the dimension named above; an argument that names none is the same for every part. Nothing has to cross between parts.
Inputs may be any that keep to these rules, and one draw needn't show every extreme that they name: `route_ids`: each row names two different experts. In the rows of one index of expert (128 aligned rows), no expert is named by more than 96 rows, a bound that some block reaches.
All inputs are finite; a program needn't handle non-finite values.
Results may differ from a plain program's by a relative error of at most 0.024.
Values may be sent and summed in bfloat16 or wider, within the bound.
A program may use at most 192 MiB of HBM per device.

v0:
```python
import jax
import jax.numpy as jnp
from jax import lax
from jax.sharding import PartitionSpec as P

CAP = 96


def shards(tokens, route_ids, gate_weights, w_gate, w_up, w_down):
    cycle_size = lax.axis_size("expert")
    token_count, local_width = tokens.shape
    slot_total = cycle_size * CAP
    expert_iota = lax.broadcasted_iota(jnp.int32, (1, 1, cycle_size), 2)
    hit_mask = route_ids[:, :, None] == expert_iota
    routed = jnp.any(hit_mask, axis=1).astype(jnp.int32)
    weighting = jnp.sum(jnp.where(hit_mask, gate_weights[:, :, None], 0.0), axis=1)
    slot_index = jnp.cumsum(routed, axis=0) - 1
    expert_base = lax.broadcasted_iota(jnp.int32, (1, cycle_size), 1) * CAP
    target_slot = jnp.where(routed == 1, expert_base + slot_index, -1)
    slot_iota = lax.broadcasted_iota(jnp.int32, (1, 1, slot_total), 2)
    pick_table = target_slot[:, :, None] == slot_iota
    select_table = jnp.any(pick_table, axis=1).astype(jnp.bfloat16)
    combine_table = jnp.sum(jnp.where(pick_table, weighting[:, :, None], 0.0), axis=1)
    dispatched = jnp.dot(select_table.T, tokens, preferred_element_type=jnp.float32)
    dispatched = dispatched.astype(jnp.bfloat16).reshape(cycle_size, CAP, local_width)
    gate_local = w_gate[0]
    up_local = w_up[0]
    down_local = w_down[0]
    received = lax.all_to_all(dispatched, "expert", split_axis=0, concat_axis=0, tiled=True)
    columns_in = lax.all_gather(
        received.reshape(slot_total, local_width), "etp", axis=1, tiled=True
    )
    gate_sum = jnp.dot(columns_in, gate_local, preferred_element_type=jnp.float32)
    up_sum = jnp.dot(columns_in, up_local, preferred_element_type=jnp.float32)
    hidden = (jax.nn.silu(gate_sum) * up_sum).astype(jnp.bfloat16)
    partial_out = jnp.dot(hidden, down_local, preferred_element_type=jnp.float32).astype(
        jnp.bfloat16
    )
    finished = (
        lax.psum_scatter(partial_out, "etp", scatter_dimension=1, tiled=True)
        .astype(jnp.float32)
        .astype(jnp.bfloat16)
    )
    results = lax.all_to_all(
        finished.reshape(cycle_size, CAP, local_width),
        "expert",
        split_axis=0,
        concat_axis=0,
        tiled=True,
    )
    flat_results = results.reshape(slot_total, local_width).astype(jnp.float32)
    mixed = jnp.dot(combine_table, flat_results, precision=lax.Precision.HIGHEST)
    return mixed.astype(jnp.bfloat16)


def solution(mesh):
    return jax.shard_map(
        shards,
        mesh=mesh,
        in_specs=(
            P(("groups", "expert"), "etp"),
            P(("groups", "expert"), None),
            P(("groups", "expert"), None),
            P("expert", None, "etp"),
            P("expert", None, "etp"),
            P("expert", "etp", None),
        ),
        out_specs=P(("groups", "expert"), "etp"),
        check_vma=False,
    )
```

profile of v0, /device:TPU:0, one launch (start us, length us, event | category | flops | bytes accessed | tf_op | source)
XLA Modules:
  0.0 231.4 jit_solution(1056805115542354805)
XLA Ops:
  6.5 0.0 copy-start
  6.5 0.0 all-gather.2.cloned.1.call-start
  6.5 0.7 fusion.18
  7.3 0.1 copy.14
  7.4 0.2 reduce_window_sum.11
  7.6 0.1 copy.15
  7.6 0.1 add_select_fusion
  7.7 0.2 fusion.17
  7.9 0.0 copy-done
  7.9 0.4 convolution_convert_fusion
  8.3 15.8 %all_to_all.10 = bf16[4,96,1024]{2,1,0:T(8,128)(2,1)} all-to-all(bf16[4,96,1024]{2,1,0:T(8,128)(2,1)S(1)} %bitcast.37), channel_id=1, replica_groups=mesh['groups'=2,'expert'=4,'etp'=4] {'expert'}, dimensions={0} | all-to-all | bytes 1572864 | tf_op jit(solution)/shard_map/all_to_all | solution.py:29
  24.1 0.0 all-gather.2.cloned.1.call-update
  24.1 0.0 reduce-scatter.2.cloned.1.call-start
  24.2 64.3 %all-gather.2.cloned.1.call-done = bf16[384,4096]{1,0:T(8,128)(2,1)} async-done(((bf16[384,1024]{1,0:T(8,128)(2,1)}), bf16[384,4096]{1,0:T(8,128)(2,1)}) %all-gather.2.cloned.1.call-update) | async-done | bytes 3145744 | tf_op jit(solution)/shard_map/all_gather | solution.py:30
  88.5 0.0 copy-start.4
  88.5 23.5 %fusion.4 = f32[384,3584]{1,0:T(8,128)} fusion(bf16[384,4096]{1,0:T(8,128)(2,1)} %all-gather.2.cloned.1.call-done, bf16[1,4096,3584]{2,1,0:T(8,128)(2,1)} %param.9), kind=kOutput, calls=%fused_computation.4 | convolution fusion | flops 11274289152 | bytes 38010880 | tf_op jit(solution)/shard_map/dot_general | solution.py:33
  112.0 0.0 copy-done.4
  112.0 18.2 %fusion.12.clone.4 = bf16[384,3584]{1,0:T(8,128)(2,1)S(1)} fusion(bf16[384,4096]{1,0:T(8,128)(2,1)S(1)} %copy-done.4, bf16[1,4096,3584]{2,1,0:T(8,128)(2,1)} %param.10, f32[384,3584]{1,0:T(8,128)} %fusion.4), kind=kOutput, calls=%fused_computation.8.clone.clone.clone.1 | convolution fusion | flops 11282546688 | bytes 40763392 | tf_op jit(solution)/shard_map/dot_general | solution.py:34
  130.2 0.0 copy-start.2
  130.2 0.0 copy-start.3
  130.2 0.0 copy-start.1
  130.2 18.7 %fusion.9 = bf16[384,4096]{1,0:T(8,128)(2,1)} fusion(bf16[1,3584,4096]{2,1,0:T(8,128)(2,1)} %param.11, bf16[384,3584]{1,0:T(8,128)(2,1)S(1)} %fusion.12.clone.4), kind=kOutput, calls=%fused_computation.7 | convolution fusion | flops 11275862016 | bytes 35258368 | tf_op jit(solution)/shard_map/dot_general | solution.py:36
  149.0 0.0 reduce-scatter.2.cloned.1.call-update
  149.0 59.2 %reduce-scatter.2.cloned.1.call-done = bf16[384,1024]{1,0:T(8,128)(2,1)} async-done(((bf16[384,4096]{1,0:T(8,128)(2,1)}), bf16[384,1024]{1,0:T(8,128)(2,1)}) %reduce-scatter.2.cloned.1.call-update) | async-done | bytes 786448 | tf_op jit(solution)/shard_map/reduce_scatter | solution.py:40
  208.2 3.5 %all-to-all-start.1 = ((bf16[4,96,1024]{2,1,0:T(8,128)(2,1)}), bf16[4,96,1024]{2,1,0:T(8,128)(2,1)S(1)}, u32[]{:S(2)}, u32[]{:S(2)}) async-start(bf16[4,96,1024]{2,1,0:T(8,128)(2,1)} %bitcast.38), calls=%async_computation.2 | async-start | bytes 1572864 | tf_op jit(solution)/shard_map/all_to_all | solution.py:44
  211.7 0.0 copy-done.2
  211.7 0.0 copy-done.3
  211.7 0.2 select_reduce_fusion
  211.9 11.3 %all-to-all-done.1 = bf16[4,96,1024]{2,1,0:T(8,128)(2,1)S(1)} async-done(((bf16[4,96,1024]{2,1,0:T(8,128)(2,1)}), bf16[4,96,1024]{2,1,0:T(8,128)(2,1)S(1)}, u32[]{:S(2)}, u32[]{:S(2)}) %all-to-all-start.1) | async-done | bytes 786464 | tf_op jit(solution)/shard_map/all_to_all | solution.py:44
  223.3 1.3 convolution_convert_fusion.1
  224.6 0.0 copy-done.1
  (3 shorter events, 0.0 us)
Async XLA Ops:
  6.5 1.4 copy-start
  6.5 81.9 %all-gather.2.cloned.1.call-start = ((), (), s32[]{:S(2)}) async-start(), calls=%async_computation.3 | async-start | bytes 3932160 | tf_op jit(solution)/shard_map/all_gather | solution.py:30
  24.1 184.1 %reduce-scatter.2.cloned.1.call-start = ((), (), s32[]{:S(2)}) async-start(), calls=%async_computation.4 | async-start | bytes 3932160 | tf_op jit(solution)/shard_map/reduce_scatter | solution.py:40
  88.5 23.5 %copy-start.4 = (bf16[384,4096]{1,0:T(8,128)(2,1)S(1)}, bf16[384,4096]{1,0:T(8,128)(2,1)}, u32[]{:S(2)}) copy-start(bf16[384,4096]{1,0:T(8,128)(2,1)} %all-gather.2.cloned.1.call-done) | copy-start | bytes 9437188
  130.2 81.5 %copy-start.2 = (f32[128,2]{0,1:T(2,128)S(1)}, f32[128,2]{0,1:T(2,128)}, u32[]{:S(2)}) copy-start(f32[128,2]{0,1:T(2,128)} %param.8) | copy-start | bytes 3076
  130.2 81.5 %copy-start.3 = (s32[128,2]{0,1:T(2,128)S(1)}, s32[128,2]{0,1:T(2,128)}, u32[]{:S(2)}) copy-start(s32[128,2]{0,1:T(2,128)} %param.7) | copy-start | bytes 3076
  130.2 94.3 %copy-start.1 = (bf16[128,1024]{1,0:T(8,128)(2,1)S(1)}, bf16[128,1024]{1,0:T(8,128)(2,1)}, u32[]{:S(2)}) copy-start(bf16[128,1024]{1,0:T(8,128)(2,1)} %param.6) | copy-start | bytes 786436
  208.2 15.1 %all-to-all-start.1 = ((bf16[4,96,1024]{2,1,0:T(8,128)(2,1)}), bf16[4,96,1024]{2,1,0:T(8,128)(2,1)S(1)}, u32[]{:S(2)}, u32[]{:S(2)}) async-start(bf16[4,96,1024]{2,1,0:T(8,128)(2,1)} %bitcast.38), calls=%async_computation.2 | async-start | bytes 1572864 | tf_op jit(solution)/shard_map/all_to_all | solution.py:44
Sparse Core Ops, SparseCore 0:
  24.2 64.1 all-gather.1
  149.1 59.0 reduce-scatter.1
where the time goes:
time: 232 us; the launch traced here: 231 us
  waiting for transfers between devices  135 us (58%)
  matrix products  62.1 us (27%)
  blocking collectives  15.8 us (7%)
  between operations  13.5 us (6%)
  starting transfers between devices  3.54 us (2%)
    all_gather x1, waiting for transfers between devices, shards(): lax.all_gather(received.reshape(slot_total, local_width), 'etp', axis=1,...  64.3 us
    reduce_scatter x1, waiting for transfers between devices, shards(): lax.psum_scatter(partial_out, 'etp', scatter_dimension=1, tiled=True)  59.2 us
    dot_general x1, matrix products, shards(): jnp.dot(columns_in, gate_local, preferred_element_type=jnp.float32)  23.5 us
    dot_general x1, matrix products, shards(): jnp.dot(hidden, down_local, preferred_element_type=jnp.float32)  18.7 us
    dot_general x1, matrix products, shards(): up_sum = jnp.dot(columns_in, up_local, preferred_element_type=jnp.float32)  18.2 us
    all_to_all x1, blocking collectives, shards(): lax.all_to_all(dispatched, 'expert', split_axis=0, concat_axis=0, tiled=T...  15.8 us
    all_to_all x1, waiting for transfers between devices, shards(): lax.all_to_all(finished.reshape(cycle_size, CAP, local_width), 'expert',...  11.3 us
  transfers between devices with their start and end apart: 3, of which 3 were waited for; matrix products, arithmetic and copies ran while one was open for 0% of the time, Pallas kernels for 0%

commit v1 on v0

--- a/solution.py
+++ b/solution.py
@@ -27,8 +27,8 @@
     up_local = w_up[0]
     down_local = w_down[0]
     received = lax.all_to_all(dispatched, "expert", split_axis=0, concat_axis=0, tiled=True)
-    columns_in = lax.all_gather(
-        received.reshape(slot_total, local_width), "etp", axis=1, tiled=True
+    columns_in = jnp.concatenate(
+        lax.all_gather(received.reshape(slot_total, local_width), "etp"), axis=1
     )
     gate_sum = jnp.dot(columns_in, gate_local, preferred_element_type=jnp.float32)
     up_sum = jnp.dot(columns_in, up_local, preferred_element_type=jnp.float32)

time: 232 us -> 230 us (level)
  matrix products: 62.1 us -> 57.3 us
  local copies, waits for them, and re-layouts: 0.2 us -> 3.62 us
    dot_general x1, matrix products: 23.5 us -> 17.8 us  [shards(): jnp.dot(columns_in, gate_local, preferred_element_type=jnp.float32)]
    all_gather x0 -> x1, local copies, waits for them, and re-layouts: none -> 3.42 us  [shards(): lax.all_gather(received.reshape(slot_total, local_width), 'etp')]
where the time goes in v1:
time: 230 us
  waiting for transfers between devices  135 us (59%)
  matrix products  57.3 us (25%)
  blocking collectives  15.8 us (7%)
  between operations  13.5 us (6%)
  local copies, waits for them, and re-layouts  3.62 us (2%)
  starting transfers between devices  3.54 us (2%)
    all_gather x1, waiting for transfers between devices, shards(): lax.all_gather(received.reshape(slot_total, local_width), 'etp')  64.3 us
    reduce_scatter x1, waiting for transfers between devices, shards(): lax.psum_scatter(partial_out, 'etp', scatter_dimension=1, tiled=True)  59.2 us
    dot_general x1, matrix products, shards(): up_sum = jnp.dot(columns_in, up_local, preferred_element_type=jnp.float32)  19 us
    dot_general x1, matrix products, shards(): jnp.dot(hidden, down_local, preferred_element_type=jnp.float32)  18.7 us
    dot_general x1, matrix products, shards(): jnp.dot(columns_in, gate_local, preferred_element_type=jnp.float32)  17.8 us
    all_to_all x1, blocking collectives, shards(): lax.all_to_all(dispatched, 'expert', split_axis=0, concat_axis=0, tiled=T...  15.8 us
    all_to_all x1, waiting for transfers between devices, shards(): lax.all_to_all(finished.reshape(cycle_size, CAP, local_width), 'expert',...  11.3 us
  transfers between devices with their start and end apart: 3, of which 3 were waited for; matrix products, arithmetic and copies ran while one was open for 0% of the time, Pallas kernels for 0%

profile of v1, /device:TPU:0, one launch (start us, length us, event | category | flops | bytes accessed | tf_op | source)
XLA Modules:
  0.0 230.0 jit_solution(14004975144004933193)
XLA Ops:
  6.5 0.0 copy-start
  6.5 0.0 all-gather.2.cloned.1.call-start
  6.5 0.7 fusion.18
  7.3 0.1 copy.24
  7.4 0.2 reduce_window_sum.11
  7.6 0.1 copy.25
  7.6 0.1 add_select_fusion
  7.7 0.2 fusion.17
  7.9 0.0 copy-done
  7.9 0.4 convolution_convert_fusion
  8.3 15.8 %all_to_all.10 = bf16[4,96,1024]{2,1,0:T(8,128)(2,1)} all-to-all(bf16[4,96,1024]{2,1,0:T(8,128)(2,1)S(1)} %bitcast.42), channel_id=1, replica_groups=mesh['groups'=2,'expert'=4,'etp'=4] {'expert'}, dimensions={0} | all-to-all | bytes 1572864 | tf_op jit(solution)/shard_map/all_to_all | solution.py:29
  24.1 0.0 all-gather.2.cloned.1.call-update
  24.1 0.0 reduce-scatter.2.cloned.1.call-start
  24.2 64.3 %all-gather.2.cloned.1.call-done = bf16[4,384,1024]{2,1,0:T(8,128)(2,1)} async-done(((bf16[1,384,1024]{2,1,0:T(8,128)(2,1)}), bf16[4,384,1024]{2,1,0:T(8,128)(2,1)}) %all-gather.2.cloned.1.call-update) | async-done | bytes 3145744 | tf_op jit(solution)/shard_map/all_gather | solution.py:31
  88.5 3.4 %copy.26 = bf16[4,384,1024]{1,2,0:T(8,128)(2,1)S(1)} copy(bf16[4,384,1024]{2,1,0:T(8,128)(2,1)} %all-gather.2.cloned.1.call-done) | data formatting | bytes 6291456 | tf_op jit(solution)/shard_map/all_gather | solution.py:31
  91.9 17.8 %fusion.4 = f32[384,3584]{1,0:T(8,128)} fusion(bf16[384,4096]{0,1:T(8,128)(2,1)S(1)} %bitcast.38, bf16[1,4096,3584]{2,1,0:T(8,128)(2,1)} %param.9), kind=kOutput, calls=%fused_computation.4 | convolution fusion | flops 11274289152 | bytes 38010880 | tf_op jit(solution)/shard_map/dot_general | solution.py:33
  109.8 19.0 %fusion.12.clone.4 = bf16[384,3584]{1,0:T(8,128)(2,1)S(1)} fusion(bf16[384,4096]{0,1:T(8,128)(2,1)S(1)} %bitcast.39, bf16[1,4096,3584]{2,1,0:T(8,128)(2,1)} %param.10, f32[384,3584]{1,0:T(8,128)} %fusion.4), kind=kOutput, calls=%fused_computation.8.clone.clone.clone.1 | convolution fusion | flops 11282546688 | bytes 40763392 | tf_op jit(solution)/shard_map/dot_general | solution.py:34
  128.8 0.0 copy-start.2
  128.8 0.0 copy-start.3
  128.8 0.0 copy-start.1
  128.8 18.7 %fusion.9 = bf16[384,4096]{1,0:T(8,128)(2,1)} fusion(bf16[1,3584,4096]{2,1,0:T(8,128)(2,1)} %param.11, bf16[384,3584]{1,0:T(8,128)(2,1)S(1)} %fusion.12.clone.4), kind=kOutput, calls=%fused_computation.7 | convolution fusion | flops 11275862016 | bytes 35258368 | tf_op jit(solution)/shard_map/dot_general | solution.py:36
  147.5 0.0 reduce-scatter.2.cloned.1.call-update
  147.5 59.2 %reduce-scatter.2.cloned.1.call-done = bf16[384,1024]{1,0:T(8,128)(2,1)} async-done(((bf16[384,4096]{1,0:T(8,128)(2,1)}), bf16[384,1024]{1,0:T(8,128)(2,1)}) %reduce-scatter.2.cloned.1.call-update) | async-done | bytes 786448 | tf_op jit(solution)/shard_map/reduce_scatter | solution.py:40
  206.8 3.5 %all-to-all-start.1 = ((bf16[4,96,1024]{2,1,0:T(8,128)(2,1)}), bf16[4,96,1024]{2,1,0:T(8,128)(2,1)S(1)}, u32[]{:S(2)}, u32[]{:S(2)}) async-start(bf16[4,96,1024]{2,1,0:T(8,128)(2,1)} %bitcast.43), calls=%async_computation.2 | async-start | bytes 1572864 | tf_op jit(solution)/shard_map/all_to_all | solution.py:44
  210.3 0.0 copy-done.2
  210.3 0.0 copy-done.3
  210.3 0.2 select_reduce_fusion
  210.5 11.3 %all-to-all-done.1 = bf16[4,96,1024]{2,1,0:T(8,128)(2,1)S(1)} async-done(((bf16[4,96,1024]{2,1,0:T(8,128)(2,1)}), bf16[4,96,1024]{2,1,0:T(8,128)(2,1)S(1)}, u32[]{:S(2)}, u32[]{:S(2)}) %all-to-all-start.1) | async-done | bytes 786464 | tf_op jit(solution)/shard_map/all_to_all | solution.py:44
  221.8 1.3 convolution_convert_fusion.1
  223.1 0.0 copy-done.1
  (3 shorter events, 0.0 us)
Async XLA Ops:
  6.5 1.4 copy-start
  6.5 82.0 %all-gather.2.cloned.1.call-start = ((), (), s32[]{:S(2)}) async-start(), calls=%async_computation.3 | async-start | bytes 3932160 | tf_op jit(solution)/shard_map/all_gather | solution.py:31
  24.1 182.6 %reduce-scatter.2.cloned.1.call-start = ((), (), s32[]{:S(2)}) async-start(), calls=%async_computation.4 | async-start | bytes 3932160 | tf_op jit(solution)/shard_map/reduce_scatter | solution.py:40
  128.8 81.5 %copy-start.2 = (f32[128,2]{0,1:T(2,128)S(1)}, f32[128,2]{0,1:T(2,128)}, u32[]{:S(2)}) copy-start(f32[128,2]{0,1:T(2,128)} %param.8) | copy-start | bytes 3076
  128.8 81.5 %copy-start.3 = (s32[128,2]{0,1:T(2,128)S(1)}, s32[128,2]{0,1:T(2,128)}, u32[]{:S(2)}) copy-start(s32[128,2]{0,1:T(2,128)} %param.7) | copy-start | bytes 3076
  128.8 94.3 %copy-start.1 = (bf16[128,1024]{1,0:T(8,128)(2,1)S(1)}, bf16[128,1024]{1,0:T(8,128)(2,1)}, u32[]{:S(2)}) copy-start(bf16[128,1024]{1,0:T(8,128)(2,1)} %param.6) | copy-start | bytes 786436
  206.8 15.1 %all-to-all-start.1 = ((bf16[4,96,1024]{2,1,0:T(8,128)(2,1)}), bf16[4,96,1024]{2,1,0:T(8,128)(2,1)S(1)}, u32[]{:S(2)}, u32[]{:S(2)}) async-start(bf16[4,96,1024]{2,1,0:T(8,128)(2,1)} %bitcast.43), calls=%async_computation.2 | async-start | bytes 1572864 | tf_op jit(solution)/shard_map/all_to_all | solution.py:44
Sparse Core Ops, SparseCore 0:
  24.2 64.2 all-gather.1
  147.7 59.0 reduce-scatter.1
